TPU v7x, 512 devices: a 8x2x16 block of a 8x8x16 slice. The times are simulated.
512 devices in a mesh: group: 2 (over y), ha: 16 (over x, core), wa: 16 (over z).
Axes of the slice: x: 8, y: 2, z: 16, core: 2. Of those that a mesh axis runs over, the one named last changes fastest.
The devices are a block of a 8x8x16 slice.
Arguments:
- queries: bfloat16 [4, 128, 128, 1536], P('group', 'ha', 'wa'), parts along dimension 0, may hold values from -6 to 6
- keys: bfloat16 [4, 128, 128, 1536], P('group', 'ha', 'wa'), parts along dimension 0, may hold values from -6 to 6
- values: bfloat16 [4, 128, 128, 1536], P('group', 'ha', 'wa'), parts along dimension 0, may hold values from -6 to 6
- out_grad: bfloat16 [4, 128, 128, 1536], P('group', 'ha', 'wa'), parts along dimension 0, may hold values from -96 to 96
- log_norm: float32 [12, 4, 128, 128], P(None, 'group', 'ha', 'wa'), parts along dimension 1, may hold values from 6.5 to 7.5
- delta_rows: float32 [12, 4, 128, 128], P(None, 'group', 'ha', 'wa'), parts along dimension 1, may hold values from -360 to 360
- text_keys: bfloat16 [64, 1536], P('group'), parts along dimension 0, may hold values from -6 to 6
- text_values: bfloat16 [64, 1536], P('group'), parts along dimension 0, may hold values from -6 to 6
- window_table: int32 [16, 16, 9], replicated, may hold values 0 or 1
Outputs:
- query_grad: bfloat16 [4, 128, 128, 1536], P('group', 'ha', 'wa'), parts along dimension 0
- key_grad: bfloat16 [4, 128, 128, 1536], P('group', 'ha', 'wa'), parts along dimension 0
- value_grad: bfloat16 [4, 128, 128, 1536], P('group', 'ha', 'wa'), parts along dimension 0
- text_key_grad: bfloat16 [64, 1536], P('group'), parts along dimension 0
- text_value_grad: bfloat16 [64, 1536], P('group'), parts along dimension 0
There are 2 independent parts, one for each index of `group`. A program takes and returns all parts, laid end to end along the dimension named above; an argument that names none is the same for every part. Nothing has to cross between parts.
All inputs are finite; a program needn't handle non-finite values.
Results may differ from a plain program's by a relative error of at most 0.001.
The roundings to bfloat16 on the way count: a program that leaves them out, or rounds other values in their place, can miss the bound.
Values may be sent and summed in bfloat16 or wider, within the bound.
A program may use at most 64 MiB of HBM per device.

v0:
```python
import math
import jax
import jax.numpy as jnp
from jax import lax
from jax.sharding import Mesh
from jax.sharding import PartitionSpec as P

HEADS = 12
HDIM = 128
TILE = 8
HALO = 2
HA = ("ha_0", "ha_1")
HA_WA = ("ha_0", "ha_1", "wa")


def passed_along(value, axis, steps):
    count = lax.axis_size(axis)
    pairs = [(source, (source + steps) % count) for source in range(count)]
    return lax.ppermute(value, axis, pairs)


def with_halo(cells, sides, width):
    for axis, dim in sides:
        count = lax.axis_size(axis)
        head = lax.slice_in_dim(cells, 0, width, axis=dim)
        tail = lax.slice_in_dim(cells, cells.shape[dim] - width, cells.shape[dim], axis=dim)
        cells = jnp.concatenate(
            [
                lax.ppermute(tail, axis, [(i, (i + 1) % count) for i in range(count)]),
                cells,
                lax.ppermute(head, axis, [((i + 1) % count, i) for i in range(count)]),
            ],
            axis=dim,
        )
    return cells


def one_axis_at_a_time(shard, axes):
    for axis in axes:
        shard = lax.psum(shard, axis)
    return shard


def tile_grads(query_rows, cotangent_rows, norm_rows, delta_part, key_rows, value_rows, cell_mask):
    score_scale = 1.0 / math.sqrt(query_rows.shape[-1])
    scores = (
        jnp.einsum("qhd,khd->hqk", query_rows, key_rows, preferred_element_type=jnp.float32)
        * score_scale
    )
    probs = jnp.exp(scores - norm_rows[:, :, None])
    if cell_mask is not None:
        probs = probs * cell_mask[None, None, :]
    probs_half = probs.astype(jnp.bfloat16)
    value_part = jnp.einsum(
        "hqk,qhd->khd", probs_half, cotangent_rows, preferred_element_type=jnp.float32
    )
    prob_grad = jnp.einsum(
        "qhd,khd->hqk", cotangent_rows, value_rows, preferred_element_type=jnp.float32
    )
    score_grad = (probs * (prob_grad - delta_part[:, :, None])).astype(jnp.bfloat16)
    query_part = (
        jnp.einsum("hqk,khd->qhd", score_grad, key_rows, preferred_element_type=jnp.float32)
        * score_scale
    )
    key_part = (
        jnp.einsum("hqk,qhd->khd", score_grad, query_rows, preferred_element_type=jnp.float32)
        * score_scale
    )
    return (query_part, key_part, value_part)


def send_cols(strip, offset):
    return passed_along(strip, "wa", offset)


def send_rows(strip, offset):
    return passed_along(strip, HA, offset)


def fold_band(buffer, along, mover):
    lower = lax.slice_in_dim(buffer, 0, HALO, axis=along)
    middle = lax.slice_in_dim(buffer, HALO, HALO + TILE, axis=along)
    upper = lax.slice_in_dim(buffer, HALO + TILE, TILE + 2 * HALO, axis=along)
    from_before = mover(upper, 1)
    from_after = mover(lower, -1)
    widths_low = [(0, 0)] * buffer.ndim
    widths_high = [(0, 0)] * buffer.ndim
    widths_low[along] = (0, TILE - HALO)
    widths_high[along] = (TILE - HALO, 0)
    return middle + jnp.pad(from_before, widths_low) + jnp.pad(from_after, widths_high)


def local(
    queries, keys, values, out_grad, log_norm, delta_rows, text_keys, text_values, window_table
):
    frames, tile_side, _, width = queries.shape
    window_side = TILE + 2 * HALO
    stacked = jnp.stack((keys, values))
    window = with_halo(stacked, ((HA, 2), ("wa", 3)), HALO)
    row_tile = lax.axis_index(HA)
    col_tile = lax.axis_index("wa")
    anchor = jnp.zeros((), jnp.int32)
    pattern = (
        lax.dynamic_slice(window_table, (row_tile, col_tile, anchor), (1, 1, 9))
        .reshape(3, 3)
        .astype(jnp.float32)
    )
    position = jnp.arange(window_side, dtype=jnp.int32)
    block_of = (position >= HALO).astype(jnp.int32) + (position >= HALO + TILE).astype(jnp.int32)
    one_hot = (block_of[:, None] == jnp.arange(3, dtype=jnp.int32)[None, :]).astype(jnp.float32)
    cell_grid = jnp.dot(
        jnp.dot(one_hot, pattern, precision=lax.Precision.HIGHEST),
        one_hot.T,
        precision=lax.Precision.HIGHEST,
    )
    cell_mask = jnp.broadcast_to(cell_grid[None], (frames, window_side, window_side)).reshape(-1)
    query_rows = queries.reshape(-1, HEADS, HDIM)
    cotangent_rows = out_grad.reshape(-1, HEADS, HDIM)
    norm_rows = log_norm.reshape(HEADS, -1)
    delta_part = delta_rows.reshape(HEADS, -1)
    key_rows = window[0].reshape(-1, HEADS, HDIM)
    value_rows = window[1].reshape(-1, HEADS, HDIM)
    video_query, video_key, video_value = tile_grads(
        query_rows, cotangent_rows, norm_rows, delta_part, key_rows, value_rows, cell_mask
    )
    text_query, text_key, text_value = tile_grads(
        query_rows,
        cotangent_rows,
        norm_rows,
        delta_part,
        text_keys.reshape(-1, HEADS, HDIM),
        text_values.reshape(-1, HEADS, HDIM),
        None,
    )
    query_grad = (
        (video_query + text_query).astype(jnp.bfloat16).reshape(frames, tile_side, tile_side, width)
    )
    text_total = one_axis_at_a_time(jnp.stack((text_key, text_value)), HA_WA)
    buffer = jnp.stack((video_key, video_value)).reshape(2, frames, window_side, window_side, width)
    buffer = fold_band(buffer, 3, send_cols)
    buffer = fold_band(buffer, 2, send_rows)
    text_key_grad = text_total[0].reshape(-1, width).astype(jnp.bfloat16)
    text_value_grad = text_total[1].reshape(-1, width).astype(jnp.bfloat16)
    return (
        query_grad,
        buffer[0].astype(jnp.bfloat16),
        buffer[1].astype(jnp.bfloat16),
        text_key_grad,
        text_value_grad,
    )


def solution(mesh):
    split = Mesh(
        mesh.devices.reshape(mesh.shape["group"], 8, 2, mesh.shape["wa"]),
        ("group", "ha_0", "ha_1", "wa"),
    )
    return jax.shard_map(
        local,
        mesh=split,
        in_specs=(
            P("group", HA, "wa", None),
            P("group", HA, "wa", None),
            P("group", HA, "wa", None),
            P("group", HA, "wa", None),
            P(None, "group", HA, "wa"),
            P(None, "group", HA, "wa"),
            P("group", None),
            P("group", None),
            P(),
        ),
        out_specs=(
            P("group", HA, "wa", None),
            P("group", HA, "wa", None),
            P("group", HA, "wa", None),
            P("group", None),
            P("group", None),
        ),
        check_vma=False,
    )
```

profile of v0, /device:TPU:71, one launch (start us, length us, event | category | flops | bytes accessed | tf_op | source)
XLA Modules:
  0.0 266.0 jit_solution(15022201213251635187)
XLA Ops:
  7.2 0.0 copy-start
  7.2 0.1 all-reduce.8.cloned.1.call-start
  7.3 1.1 pad_maximum_fusion.7
  8.4 3.1 %collective-permute-start = (bf16[2,2,2,8,1536]{4,3,2,1,0:T(8,128)(2,1)S(1)}, bf16[2,2,2,8,1536]{4,3,2,1,0:T(8,128)(2,1)S(1)}, u32[]{:S(2)}, u32[]{:S(2)}) collective-permute-start(bf16[2,2,2,8,1536]{4,3,2,1,0:T(8,128)(2,1)S(1)} %get-tuple-element.20), channel_id=1, source_target_pairs={{0,16},{16,32},{32,48},{48,64},{64,80},{80,96},{96,112},{112,128},... | collective-permute-start | bytes 589832 | tf_op jit(solution)/shard_map/ppermute | solution.py:29
  11.5 0.9 copy.34
  12.4 0.9 copy.37
  13.3 1.3 reshape.49
  14.7 0.3 reshape.50
  14.9 0.0 copy-start.4
  15.0 0.0 copy-start.5
  15.0 0.3 fusion.10
  15.3 0.2 convolution_bitcast_fusion.1
  15.5 0.3 fusion.11
  15.9 0.2 fusion.7
  16.1 0.8 pad_maximum_fusion.1
  16.9 0.1 all-reduce.8.cloned.1.call-update
  16.9 0.1 all-reduce.10.cloned.1.call-start
  17.0 1.0 convert_reduce_fusion
  18.0 0.1 convert_element_type.67
  18.1 0.0 collective-permute-done
  18.1 0.0 collective-permute-done.1
  18.1 1.1 pad_maximum_fusion.5
  19.2 5.7 %collective-permute-start.2 = (bf16[2,2,12,2,1536]{4,3,2,1,0:T(2,128)(2,1)}, bf16[2,2,12,2,1536]{4,3,2,1,0:T(2,128)(2,1)S(1)}, u32[]{:S(2)}, u32[]{:S(2)}) collective-permute-start(bf16[2,2,12,2,1536]{4,3,2,1,0:T(2,128)(2,1)} %get-tuple-element.16), channel_id=1, source_target_pairs={{0,1},{1,2},{2,3},{3,4},{4,5},{5,6},{6,7},{7,8},{8,9},{9,10},{10,1... | collective-permute-start | bytes 884744 | tf_op jit(solution)/shard_map/ppermute | solution.py:29
  25.0 39.9 %collective-permute-start.3 = (bf16[2,2,12,2,1536]{4,3,2,1,0:T(2,128)(2,1)S(1)}, bf16[2,2,12,2,1536]{4,3,2,1,0:T(2,128)(2,1)S(1)}, u32[]{:S(2)}, u32[]{:S(2)}) collective-permute-start(bf16[2,2,12,2,1536]{4,3,2,1,0:T(2,128)(2,1)S(1)} %get-tuple-element.17), channel_id=1, source_target_pairs={{1,0},{2,1},{3,2},{4,3},{5,4},{6,5},{7,6},{8,7},{9,8},{10,9},{11,1... | collective-permute-start | bytes 884744 | tf_op jit(solution)/shard_map/ppermute | solution.py:31
  64.9 0.2 fusion.32
  65.1 0.2 fusion.31
  65.3 0.1 mul.66
  65.4 65.5 %all-reduce.8.cloned.1.call-done = f32[2,32,12,128]{3,1,2,0:T(8,128)} async-done(((f32[2,32,12,128]{3,1,2,0:T(8,128)}), f32[2,32,12,128]{3,1,2,0:T(8,128)}) %all-reduce.8.cloned.1.call-update) | async-done | bytes 393232 | tf_op jit(solution)/shard_map/psum | solution.py:40
  130.9 0.1 all-reduce.10.cloned.1.call-update
  131.0 0.0 collective-permute-done.2
  131.0 1.5 pad_maximum_fusion
  132.5 0.2 fusion.38
  132.7 1.7 reshape_squeeze.9
  134.3 0.8 reshape_squeeze.8
  135.2 0.6 exponential_multiply_fusion
  135.8 1.6 convolution_bitcast_fusion
  137.4 0.5 multiply_convert_fusion
  137.9 0.0 copy-start.7
  137.9 0.6 fusion.5
  138.5 0.4 multiply_bitcast_fusion
  138.9 0.3 fusion.6
  139.2 0.4 copy.48
  139.6 1.0 reshape.53
  140.6 2.5 copy.50
  143.1 2.4 stack.30
  145.5 4.0 %copy.52 = f32[288,12,128]{2,1,0:T(8,128)} copy(f32[288,12,128]{2,0,1:T(8,128)} %convolution_bitcast_fusion) | data formatting | bytes 3538944 | tf_op jit(solution)/shard_map/hqk,qhd->khd/transpose | solution.py:54
  149.5 3.2 %stack.31 = f32[1,2,12,12,1536]{4,3,2,1,0:T(8,128)} reshape(f32[288,12,128]{2,1,0:T(8,128)} %copy.52) | data formatting | bytes 3538944 | tf_op jit(solution)/shard_map/stack | solution.py:139
  152.7 0.2 constant_dynamic-update-slice_fusion.1
  152.9 1.4 copy-done.1
  154.4 0.2 constant_dynamic-update-slice_fusion
  154.5 2.1 copy-done.2
  156.7 0.5 fusion.36
  157.2 3.3 %collective-permute-start.4 = (f32[2,2,12,2,1536]{4,3,2,1,0:T(2,128)S(1)}, f32[2,2,12,2,1536]{4,3,2,1,0:T(2,128)S(1)}, u32[]{:S(2)}, u32[]{:S(2)}) collective-permute-start(f32[2,2,12,2,1536]{4,3,2,1,0:T(2,128)S(1)} %get-tuple-element.10), channel_id=1, source_target_pairs={{0,1},{1,2},{2,3},{3,4},{4,5},{5,6},{6,7},{7,8},{8,9},{9,10},{10,1... | collective-permute-start | bytes 1769480 | tf_op jit(solution)/shard_map/ppermute | solution.py:19
  160.5 5.5 %collective-permute-start.5 = (f32[2,2,12,2,1536]{4,3,2,1,0:T(2,128)S(1)}, f32[2,2,12,2,1536]{4,3,2,1,0:T(2,128)S(1)}, u32[]{:S(2)}, u32[]{:S(2)}) collective-permute-start(f32[2,2,12,2,1536]{4,3,2,1,0:T(2,128)S(1)} %get-tuple-element.11), channel_id=1, source_target_pairs={{0,15},{1,0},{2,1},{3,2},{4,3},{5,4},{6,5},{7,6},{8,7},{9,8},{10,9... | collective-permute-start | bytes 1769480 | tf_op jit(solution)/shard_map/ppermute | solution.py:19
  166.0 15.4 %all-reduce.10.cloned.1.call-done = f32[2,32,12,128]{3,1,2,0:T(8,128)} async-done(((f32[2,32,12,128]{3,1,2,0:T(8,128)}), f32[2,32,12,128]{3,1,2,0:T(8,128)}) %all-reduce.10.cloned.1.call-update) | async-done | bytes 393232 | tf_op jit(solution)/shard_map/psum | solution.py:40
  181.4 48.9 %all-reduce.11 = bf16[2,32,12,128]{3,1,2,0:T(8,128)(2,1)S(1)} all-reduce(f32[2,32,12,128]{3,1,2,0:T(8,128)} %all-reduce.10.cloned.1.call-done), channel_id=1, replica_groups=mesh['group'=2,'ha_0'=8,'ha_1'=2,'wa'=16] {'wa'}, use_global_device_ids=true, to_apply=%region_2.0 | all-reduce | flops 98304 | bytes 589824 | tf_op jit(solution)/shard_map/psum | solution.py:40
  230.4 3.0 %fusion = f32[2,2,12,8,1536]{4,3,2,1,0:T(8,128)S(1)} fusion(f32[2,2,12,12,1536]{4,3,2,1,0:T(8,128)} %copy-done.2, f32[2,2,12,2,1536]{4,3,2,1,0:T(2,128)S(1)} %collective-permute-done.5, f32[2,2,12,2,1536]{4,3,2,1,0:T(2,128)S(1)} %collective-permute-done.4), kind=kLoop, calls=%fused_computation.1 | loop fusion | flops 1179648 | bytes 5898240 | tf_op jit(solution)/shard_map/add | solution.py:90
  233.4 0.1 fusion.37
  233.5 16.2 %collective-permute-start.6 = (f32[2,2,2,8,1536]{4,3,2,1,0:T(8,128)S(1)}, f32[2,2,2,8,1536]{4,3,2,1,0:T(8,128)S(1)}, u32[]{:S(2)}, u32[]{:S(2)}) collective-permute-start(f32[2,2,2,8,1536]{4,3,2,1,0:T(8,128)S(1)} %get-tuple-element.12), channel_id=1, source_target_pairs={{0,16},{16,32},{32,48},{48,64},{64,80},{80,96},{96,112},{112,128},... | collective-permute-start | bytes 1179656 | tf_op jit(solution)/shard_map/ppermute | solution.py:19
  249.7 0.7 copy_bitcast_fusion
  250.4 4.0 %collective-permute-done.6 = f32[2,2,2,8,1536]{4,3,2,1,0:T(8,128)S(1)} collective-permute-done((f32[2,2,2,8,1536]{4,3,2,1,0:T(8,128)S(1)}, f32[2,2,2,8,1536]{4,3,2,1,0:T(8,128)S(1)}, u32[]{:S(2)}, u32[]{:S(2)}) %collective-permute-start.6) | collective-permute-done | bytes 393248 | tf_op jit(solution)/shard_map/ppermute | solution.py:19
  254.4 3.7 %collective-permute-done.7 = f32[2,2,2,8,1536]{4,3,2,1,0:T(8,128)S(1)} collective-permute-done((f32[2,2,2,8,1536]{4,3,2,1,0:T(8,128)S(1)}, f32[2,2,2,8,1536]{4,3,2,1,0:T(8,128)S(1)}, u32[]{:S(2)}, u32[]{:S(2)}) %collective-permute-start.7) | collective-permute-done | bytes 393248 | tf_op jit(solution)/shard_map/ppermute | solution.py:19
  258.1 0.2 fusion.2
  258.2 0.9 slice_bitcast_fusion
  (24 shorter events, 0.2 us)
Async XLA Ops:
  7.2 7.8 %copy-start = (bf16[32,1536]{1,0:T(8,128)(2,1)S(1)}, bf16[32,1536]{1,0:T(8,128)(2,1)}, u32[]{:S(2)}) copy-start(bf16[32,1536]{1,0:T(8,128)(2,1)} %param.15) | copy-start | bytes 294916
  7.2 7.4 %copy-start.8 = (bf16[2,8,8,1536]{3,2,1,0:T(8,128)(2,1)S(1)}, bf16[2,8,8,1536]{3,2,1,0:T(8,128)(2,1)}, u32[]{:S(2)}) copy-start(bf16[2,8,8,1536]{3,2,1,0:T(8,128)(2,1)} %param.12) | copy-start | bytes 1179652
  7.2 123.7 %all-reduce.8.cloned.1.call-start = ((), (), s32[]{:S(2)}) async-start(), calls=%async_computation | async-start | bytes 786432 | tf_op jit(solution)/shard_map/psum | solution.py:40
  7.3 8.3 %copy-start.9 = (bf16[32,1536]{1,0:T(8,128)(2,1)S(1)}, bf16[32,1536]{1,0:T(8,128)(2,1)}, u32[]{:S(2)}) copy-start(bf16[32,1536]{1,0:T(8,128)(2,1)} %param.16) | copy-start | bytes 294916
  8.4 9.7 %collective-permute-start = (bf16[2,2,2,8,1536]{4,3,2,1,0:T(8,128)(2,1)S(1)}, bf16[2,2,2,8,1536]{4,3,2,1,0:T(8,128)(2,1)S(1)}, u32[]{:S(2)}, u32[]{:S(2)}) collective-permute-start(bf16[2,2,2,8,1536]{4,3,2,1,0:T(8,128)(2,1)S(1)} %get-tuple-element.20), channel_id=1, source_target_pairs={{0,16},{16,32},{32,48},{48,64},{64,80},{80,96},{96,112},{112,128},... | collective-permute-start | bytes 589832 | tf_op jit(solution)/shard_map/ppermute | solution.py:29
  11.5 6.6 %collective-permute-start.1 = (bf16[2,2,2,8,1536]{4,3,2,1,0:T(8,128)(2,1)S(1)}, bf16[2,2,2,8,1536]{4,3,2,1,0:T(8,128)(2,1)S(1)}, u32[]{:S(2)}, u32[]{:S(2)}) collective-permute-start(bf16[2,2,2,8,1536]{4,3,2,1,0:T(8,128)(2,1)S(1)} %get-tuple-element.21), channel_id=1, source_target_pairs={{16,0},{32,16},{48,32},{64,48},{80,64},{96,80},{112,96},{128,112},... | collective-permute-start | bytes 589832 | tf_op jit(solution)/shard_map/ppermute | solution.py:31
  14.9 3.2 %copy-start.4 = (bf16[2,8,8,1536]{3,2,1,0:T(8,128)(2,1)S(1)}, bf16[2,8,8,1536]{3,2,1,0:T(8,128)(2,1)}, u32[]{:S(2)}) copy-start(bf16[2,8,8,1536]{3,2,1,0:T(8,128)(2,1)} %param.11) | copy-start | bytes 1179652
  15.0 3.2 %copy-start.5 = (bf16[2,8,8,1536]{3,2,1,0:T(8,128)(2,1)S(1)}, bf16[2,8,8,1536]{3,2,1,0:T(8,128)(2,1)}, u32[]{:S(2)}) copy-start(bf16[2,8,8,1536]{3,2,1,0:T(8,128)(2,1)} %param.10) | copy-start | bytes 1179652
  15.9 115.2 %copy-start.6 = (bf16[12,128,32]{1,2,0:T(8,128)(2,1)}, bf16[12,128,32]{1,2,0:T(8,128)(2,1)S(1)}, u32[]{:S(2)}) copy-start(bf16[12,128,32]{1,2,0:T(8,128)(2,1)S(1)} %fusion.11) | copy-start | bytes 294916
  16.9 164.4 %all-reduce.10.cloned.1.call-start = ((), (), s32[]{:S(2)}) async-start(), calls=%async_computation.1 | async-start | bytes 786432 | tf_op jit(solution)/shard_map/psum | solution.py:40
  19.2 111.8 %collective-permute-start.2 = (bf16[2,2,12,2,1536]{4,3,2,1,0:T(2,128)(2,1)}, bf16[2,2,12,2,1536]{4,3,2,1,0:T(2,128)(2,1)S(1)}, u32[]{:S(2)}, u32[]{:S(2)}) collective-permute-start(bf16[2,2,12,2,1536]{4,3,2,1,0:T(2,128)(2,1)} %get-tuple-element.16), channel_id=1, source_target_pairs={{0,1},{1,2},{2,3},{3,4},{4,5},{5,6},{6,7},{7,8},{8,9},{9,10},{10,1... | collective-permute-start | bytes 884744 | tf_op jit(solution)/shard_map/ppermute | solution.py:29
  25.0 106.0 %collective-permute-start.3 = (bf16[2,2,12,2,1536]{4,3,2,1,0:T(2,128)(2,1)S(1)}, bf16[2,2,12,2,1536]{4,3,2,1,0:T(2,128)(2,1)S(1)}, u32[]{:S(2)}, u32[]{:S(2)}) collective-permute-start(bf16[2,2,12,2,1536]{4,3,2,1,0:T(2,128)(2,1)S(1)} %get-tuple-element.17), channel_id=1, source_target_pairs={{1,0},{2,1},{3,2},{4,3},{5,4},{6,5},{7,6},{8,7},{9,8},{10,9},{11,1... | collective-permute-start | bytes 884744 | tf_op jit(solution)/shard_map/ppermute | solution.py:31
  135.8 1.6 copy-start.3
  137.9 1.0 copy-start.7
  152.7 1.7 copy-start.1
  154.5 2.1 copy-start.2
  157.2 73.2 %collective-permute-start.4 = (f32[2,2,12,2,1536]{4,3,2,1,0:T(2,128)S(1)}, f32[2,2,12,2,1536]{4,3,2,1,0:T(2,128)S(1)}, u32[]{:S(2)}, u32[]{:S(2)}) collective-permute-start(f32[2,2,12,2,1536]{4,3,2,1,0:T(2,128)S(1)} %get-tuple-element.10), channel_id=1, source_target_pairs={{0,1},{1,2},{2,3},{3,4},{4,5},{5,6},{6,7},{7,8},{8,9},{9,10},{10,1... | collective-permute-start | bytes 1769480 | tf_op jit(solution)/shard_map/ppermute | solution.py:19
  160.5 69.9 %collective-permute-start.5 = (f32[2,2,12,2,1536]{4,3,2,1,0:T(2,128)S(1)}, f32[2,2,12,2,1536]{4,3,2,1,0:T(2,128)S(1)}, u32[]{:S(2)}, u32[]{:S(2)}) collective-permute-start(f32[2,2,12,2,1536]{4,3,2,1,0:T(2,128)S(1)} %get-tuple-element.11), channel_id=1, source_target_pairs={{0,15},{1,0},{2,1},{3,2},{4,3},{5,4},{6,5},{7,6},{8,7},{9,8},{10,9... | collective-permute-start | bytes 1769480 | tf_op jit(solution)/shard_map/ppermute | solution.py:19
  233.5 20.9 %collective-permute-start.6 = (f32[2,2,2,8,1536]{4,3,2,1,0:T(8,128)S(1)}, f32[2,2,2,8,1536]{4,3,2,1,0:T(8,128)S(1)}, u32[]{:S(2)}, u32[]{:S(2)}) collective-permute-start(f32[2,2,2,8,1536]{4,3,2,1,0:T(8,128)S(1)} %get-tuple-element.12), channel_id=1, source_target_pairs={{0,16},{16,32},{32,48},{48,64},{64,80},{80,96},{96,112},{112,128},... | collective-permute-start | bytes 1179656 | tf_op jit(solution)/shard_map/ppermute | solution.py:19
  249.7 8.4 %collective-permute-start.7 = (f32[2,2,2,8,1536]{4,3,2,1,0:T(8,128)S(1)}, f32[2,2,2,8,1536]{4,3,2,1,0:T(8,128)S(1)}, u32[]{:S(2)}, u32[]{:S(2)}) collective-permute-start(f32[2,2,2,8,1536]{4,3,2,1,0:T(8,128)S(1)} %get-tuple-element.13), channel_id=1, source_target_pairs={{0,240},{16,0},{32,16},{48,32},{64,48},{80,64},{96,80},{112,96},{1... | collective-permute-start | bytes 1179656 | tf_op jit(solution)/shard_map/ppermute | solution.py:19
Sparse Core Ops, SparseCore 0:
  17.1 113.8 all-reduce.7
  133.8 47.4 all-reduce.9
where the time goes:
time: 267 us; the launch traced here: 266 us
  waiting for transfers between devices  88.7 us (33%)
  starting transfers between devices  73.8 us (28%)
  blocking collectives  48.9 us (18%)
  local copies, waits for them, and re-layouts  26 us (10%)
  between operations  14.4 us (5%)
  other arithmetic  8.7 us (3%)
  matrix products  5.43 us (2%)
    psum x2, waiting for transfers between devices, one_axis_at_a_time(): shard = lax.psum(shard, axis)  80.9 us
    psum x1, blocking collectives, one_axis_at_a_time(): shard = lax.psum(shard, axis)  48.9 us
    ppermute x2, starting transfers between devices, with_halo(): lax.ppermute(head, axis, [((i + 1) % count, i) for i in range(count)])  39.9 us
    ppermute x4, starting transfers between devices, passed_along(): return lax.ppermute(value, axis, pairs)  24.9 us
    ppermute x2, starting transfers between devices, with_halo(): lax.ppermute(tail, axis, [(i, (i + 1) % count) for i in range(count)])  8.83 us
    ppermute x4, waiting for transfers between devices, passed_along(): return lax.ppermute(value, axis, pairs)  7.7 us
    another operation x3, local copies, waits for them, and re-layouts, local(): jnp.stack((video_key, video_value))  5.77 us
  transfers between devices with their start and end apart: 10, of which 4 were waited for; matrix products, arithmetic and copies ran while one was open for 12% of the time, Pallas kernels for 0%

commit v1 on v0

--- a/solution.py
+++ b/solution.py
@@ -37,7 +37,7 @@
 
 def one_axis_at_a_time(shard, axes):
     for axis in axes:
-        shard = lax.psum(shard, axis)
+        shard = lax.all_gather(shard, axis).sum(axis=0)
     return shard
 
 

time: 267 us -> 219 us (0.82)
  the two profiles are of different devices: /device:TPU:71 before, /device:TPU:66 now
where the time goes in v1:
time: 219 us; the launch traced here: 218 us
  waiting for transfers between devices  136 us (62%)
  local copies, waits for them, and re-layouts  26.9 us (12%)
  starting transfers between devices  20.6 us (9%)
  between operations  14.4 us (7%)
  other arithmetic  12.3 us (6%)
  matrix products  5.71 us (3%)
  blocking collectives  2.42 us (1%)
    all_gather x2, waiting for transfers between devices, one_axis_at_a_time(): shard = lax.all_gather(shard, axis).sum(axis=0)  94.4 us
    ppermute x4, waiting for transfers between devices, passed_along(): return lax.ppermute(value, axis, pairs)  28.9 us
    ppermute x4, starting transfers between devices, passed_along(): return lax.ppermute(value, axis, pairs)  9.61 us
    ppermute x2, starting transfers between devices, with_halo(): lax.ppermute(head, axis, [((i + 1) % count, i) for i in range(count)])  7.08 us
    ppermute x2, waiting for transfers between devices, with_halo(): lax.ppermute(tail, axis, [(i, (i + 1) % count) for i in range(count)])  6.7 us
    reduce_sum x3, other arithmetic, one_axis_at_a_time(): shard = lax.all_gather(shard, axis).sum(axis=0)  6.66 us
    another operation x3, local copies, waits for them, and re-layouts, local(): jnp.stack((video_key, video_value))  5.85 us
    ppermute x2, waiting for transfers between devices, with_halo(): lax.ppermute(head, axis, [((i + 1) % count, i) for i in range(count)])  5.67 us
  transfers between devices with their start and end apart: 10, of which 8 were waited for; matrix products, arithmetic and copies ran while one was open for 12% of the time, Pallas kernels for 0%

profile of v1, /device:TPU:66, one launch (start us, length us, event | category | flops | bytes accessed | tf_op | source)
XLA Modules:
  0.0 218.0 jit_solution(18182901159024862926)
XLA Ops:
  7.3 0.9 copy.80
  8.2 0.9 copy.83
  9.1 1.3 reshape.49
  10.4 1.3 reshape.50
  11.7 0.3 fusion.10
  12.1 0.2 convolution_bitcast_fusion.1
  12.3 0.3 fusion.11
  12.6 0.7 copy-done.10
  13.3 0.2 fusion.7
  13.5 0.8 pad_maximum_fusion.1
  14.4 84.6 %all-gather.6.cloned.1.call-done = f32[16,32,12,128]{3,1,2,0:T(8,128)} async-done(((f32[2,32,12,128]{3,1,2,0:T(8,128)}), f32[16,32,12,128]{3,1,2,0:T(8,128)}) %all-gather.6.cloned.1.call-update) | async-done | bytes 3145744 | tf_op jit(solution)/shard_map/all_gather | solution.py:40
  99.0 2.3 %reduce_sum.27 = f32[2,32,12,128]{3,1,2,0:T(8,128)S(1)} reduce(f32[8,2,32,12,128]{4,2,3,1,0:T(8,128)} %bitcast.76, f32[]{:T(128)} %constant.32.clone.1), dimensions={0}, to_apply=%region_0.0 | reduce | flops 688128 | bytes 3538948 | tf_op jit(solution)/shard_map/reduce_sum | solution.py:40
  101.3 2.4 %all-gather.1 = f32[4,32,12,128]{3,1,2,0:T(8,128)S(1)} all-gather(f32[2,32,12,128]{3,1,2,0:T(8,128)S(1)} %reduce_sum.27), channel_id=3, replica_groups=mesh['group'=2,'ha_0'=8,'ha_1'=2,'wa'=16] {'ha_1'}, dimensions={0}, use_global_device_ids=true | all-gather | bytes 1179648 | tf_op jit(solution)/shard_map/all_gather | solution.py:40
  103.7 0.8 reduce_sum.28
  104.7 0.2 collective-permute-start
  104.8 1.6 collective-permute-start.1
  106.4 1.0 convert_reduce_fusion
  107.4 0.1 convert_element_type.67
  107.5 2.3 %collective-permute-done = bf16[2,2,2,8,1536]{4,3,2,1,0:T(8,128)(2,1)S(1)} collective-permute-done((bf16[2,2,2,8,1536]{4,3,2,1,0:T(8,128)(2,1)S(1)}, bf16[2,2,2,8,1536]{4,3,2,1,0:T(8,128)(2,1)S(1)}, u32[]{:S(2)}, u32[]{:S(2)}) %collective-permute-start) | collective-permute-done | bytes 196640 | tf_op jit(solution)/shard_map/ppermute | solution.py:29
  109.8 0.4 pad_maximum_fusion.5
  110.2 3.6 %collective-permute-start.2 = (bf16[2,2,12,2,1536]{4,3,2,1,0:T(2,128)(2,1)S(1)}, bf16[2,2,12,2,1536]{4,3,2,1,0:T(2,128)(2,1)S(1)}, u32[]{:S(2)}, u32[]{:S(2)}) collective-permute-start(bf16[2,2,12,2,1536]{4,3,2,1,0:T(2,128)(2,1)S(1)} %get-tuple-element.16), channel_id=1, source_target_pairs={{0,1},{1,2},{2,3},{3,4},{4,5},{5,6},{6,7},{7,8},{8,9},{9,10},{10,1... | collective-permute-start | bytes 884744 | tf_op jit(solution)/shard_map/ppermute | solution.py:29
  113.8 5.5 %collective-permute-start.3 = (bf16[2,2,12,2,1536]{4,3,2,1,0:T(2,128)(2,1)S(1)}, bf16[2,2,12,2,1536]{4,3,2,1,0:T(2,128)(2,1)S(1)}, u32[]{:S(2)}, u32[]{:S(2)}) collective-permute-start(bf16[2,2,12,2,1536]{4,3,2,1,0:T(2,128)(2,1)S(1)} %get-tuple-element.17), channel_id=1, source_target_pairs={{1,0},{2,1},{3,2},{4,3},{5,4},{6,5},{7,6},{8,7},{9,8},{10,9},{11,1... | collective-permute-start | bytes 884744 | tf_op jit(solution)/shard_map/ppermute | solution.py:31
  119.2 0.2 fusion.32
  119.4 0.2 fusion.31
  119.6 0.1 mul.66
  119.8 4.4 %collective-permute-done.2 = bf16[2,2,12,2,1536]{4,3,2,1,0:T(2,128)(2,1)S(1)} collective-permute-done((bf16[2,2,12,2,1536]{4,3,2,1,0:T(2,128)(2,1)S(1)}, bf16[2,2,12,2,1536]{4,3,2,1,0:T(2,128)(2,1)S(1)}, u32[]{:S(2)}, u32[]{:S(2)}) %collective-permute-start.2) | collective-permute-done | bytes 294944 | tf_op jit(solution)/shard_map/ppermute | solution.py:29
  124.2 5.7 %collective-permute-done.3 = bf16[2,2,12,2,1536]{4,3,2,1,0:T(2,128)(2,1)S(1)} collective-permute-done((bf16[2,2,12,2,1536]{4,3,2,1,0:T(2,128)(2,1)S(1)}, bf16[2,2,12,2,1536]{4,3,2,1,0:T(2,128)(2,1)S(1)}, u32[]{:S(2)}, u32[]{:S(2)}) %collective-permute-start.3) | collective-permute-done | bytes 294944 | tf_op jit(solution)/shard_map/ppermute | solution.py:31
  129.8 1.5 pad_maximum_fusion
  131.3 0.2 fusion.38
  131.5 1.6 reshape_squeeze.9
  133.1 0.8 reshape_squeeze.8
  134.0 0.6 exponential_multiply_fusion
  134.5 1.1 copy-done.7
  135.6 0.5 multiply_convert_fusion
  136.1 0.4 multiply_bitcast_fusion
  136.5 0.4 copy-done.4
  136.9 0.3 copy-done.2
  137.2 2.5 %copy.96 = f32[288,12,128]{2,1,0:T(8,128)} copy(f32[288,12,128]{2,0,1:T(8,128)S(1)} %multiply_bitcast_fusion) | data formatting | bytes 3538944 | tf_op jit(solution)/shard_map/mul | solution.py:66
  139.7 2.4 %stack.30 = f32[1,2,12,12,1536]{4,3,2,1,0:T(8,128)S(1)} reshape(f32[288,12,128]{2,1,0:T(8,128)} %copy.96) | data formatting | bytes 3538944 | tf_op jit(solution)/shard_map/stack | solution.py:139
  142.1 1.9 convolution_bitcast_fusion
  144.0 2.6 %copy.98 = f32[288,12,128]{2,1,0:T(8,128)} copy(f32[288,12,128]{2,0,1:T(8,128)S(1)} %convolution_bitcast_fusion) | data formatting | bytes 3538944 | tf_op jit(solution)/shard_map/hqk,qhd->khd/transpose | solution.py:54
  146.6 3.2 %stack.31 = f32[1,2,12,12,1536]{4,3,2,1,0:T(8,128)} reshape(f32[288,12,128]{2,1,0:T(8,128)} %copy.98) | data formatting | bytes 3538944 | tf_op jit(solution)/shard_map/stack | solution.py:139
  149.8 0.2 constant_dynamic-update-slice_fusion.1
  150.0 1.5 copy-done.1
  151.5 0.2 constant_dynamic-update-slice_fusion
  151.7 0.5 fusion.36
  152.3 2.0 collective-permute-start.4
  154.2 5.9 %collective-permute-start.5 = (f32[2,2,12,2,1536]{4,3,2,1,0:T(2,128)S(1)}, f32[2,2,12,2,1536]{4,3,2,1,0:T(2,128)S(1)}, u32[]{:S(2)}, u32[]{:S(2)}) collective-permute-start(f32[2,2,12,2,1536]{4,3,2,1,0:T(2,128)S(1)} %get-tuple-element.11), channel_id=1, source_target_pairs={{0,15},{1,0},{2,1},{3,2},{4,3},{5,4},{6,5},{7,6},{8,7},{9,8},{10,9... | collective-permute-start | bytes 1769480 | tf_op jit(solution)/shard_map/ppermute | solution.py:19
  160.2 23.9 %collective-permute-done.4 = f32[2,2,12,2,1536]{4,3,2,1,0:T(2,128)S(1)} collective-permute-done((f32[2,2,12,2,1536]{4,3,2,1,0:T(2,128)S(1)}, f32[2,2,12,2,1536]{4,3,2,1,0:T(2,128)S(1)}, u32[]{:S(2)}, u32[]{:S(2)}) %collective-permute-start.4) | collective-permute-done | bytes 589856 | tf_op jit(solution)/shard_map/ppermute | solution.py:19
  184.0 1.7 collective-permute-done.5
  185.7 0.7 fusion
  186.4 1.0 fusion.37
  187.3 1.2 collective-permute-start.6
  188.6 0.5 collective-permute-start.7
  189.1 0.6 fusion.5
  189.7 0.3 fusion.6
  190.0 0.4 copy.94
  190.4 1.0 reshape.53
  191.4 3.4 %collective-permute-done.6 = f32[2,2,2,8,1536]{4,3,2,1,0:T(8,128)} collective-permute-done((f32[2,2,2,8,1536]{4,3,2,1,0:T(8,128)}, f32[2,2,2,8,1536]{4,3,2,1,0:T(8,128)}, u32[]{:S(2)}, u32[]{:S(2)}) %collective-permute-start.6) | collective-permute-done | bytes 393248 | tf_op jit(solution)/shard_map/ppermute | solution.py:19
  194.9 1.3 fusion.2
  196.1 0.9 slice_bitcast_fusion
  197.0 9.8 %all-gather.8.cloned.1.call-done = f32[32,32,12,128]{3,1,2,0:T(8,128)} async-done(((f32[2,32,12,128]{3,1,2,0:T(8,128)}), f32[32,32,12,128]{3,1,2,0:T(8,128)}) %all-gather.8.cloned.1.call-update) | async-done | bytes 6291472 | tf_op jit(solution)/shard_map/all_gather | solution.py:40
  206.8 3.5 %reduce_sum.29 = bf16[2,32,12,128]{3,1,2,0:T(8,128)(2,1)S(1)} reduce(f32[16,2,32,12,128]{4,2,3,1,0:T(8,128)} %bitcast.68, f32[]{:T(128)} %constant.32.clone.1), dimensions={0}, to_apply=%region_2.0 | reduce | flops 1474560 | bytes 6488068 | tf_op jit(solution)/shard_map/reduce_sum | solution.py:40
  210.5 0.7 copy_bitcast_fusion
  (33 shorter events, 0.4 us)
Async XLA Ops:
  7.2 4.5 %copy-start = (bf16[32,1536]{1,0:T(8,128)(2,1)S(1)}, bf16[32,1536]{1,0:T(8,128)(2,1)}, u32[]{:S(2)}) copy-start(bf16[32,1536]{1,0:T(8,128)(2,1)} %param.15) | copy-start | bytes 294916
  7.2 5.1 %copy-start.12 = (bf16[32,1536]{1,0:T(8,128)(2,1)S(1)}, bf16[32,1536]{1,0:T(8,128)(2,1)}, u32[]{:S(2)}) copy-start(bf16[32,1536]{1,0:T(8,128)(2,1)} %param.16) | copy-start | bytes 294916
  7.2 91.7 %all-gather.6.cloned.1.call-start = ((), (), s32[]{:S(2)}) async-start(), calls=%async_computation | async-start | bytes 3538944 | tf_op jit(solution)/shard_map/all_gather | solution.py:40
  12.6 0.7 copy-start.10
  14.3 192.5 %all-gather.8.cloned.1.call-start = ((), (), s32[]{:S(2)}) async-start(), calls=%async_computation.1 | async-start | bytes 6684672 | tf_op jit(solution)/shard_map/all_gather | solution.py:40
  98.9 5.6 %copy-start.8 = (bf16[2,8,8,1536]{3,2,1,0:T(8,128)(2,1)S(1)}, bf16[2,8,8,1536]{3,2,1,0:T(8,128)(2,1)}, u32[]{:S(2)}) copy-start(bf16[2,8,8,1536]{3,2,1,0:T(8,128)(2,1)} %param.11) | copy-start | bytes 1179652
  98.9 5.7 %copy-start.9 = (bf16[2,8,8,1536]{3,2,1,0:T(8,128)(2,1)S(1)}, bf16[2,8,8,1536]{3,2,1,0:T(8,128)(2,1)}, u32[]{:S(2)}) copy-start(bf16[2,8,8,1536]{3,2,1,0:T(8,128)(2,1)} %param.10) | copy-start | bytes 1179652
  104.7 5.1 %collective-permute-start = (bf16[2,2,2,8,1536]{4,3,2,1,0:T(8,128)(2,1)S(1)}, bf16[2,2,2,8,1536]{4,3,2,1,0:T(8,128)(2,1)S(1)}, u32[]{:S(2)}, u32[]{:S(2)}) collective-permute-start(bf16[2,2,2,8,1536]{4,3,2,1,0:T(8,128)(2,1)S(1)} %get-tuple-element.20), channel_id=1, source_target_pairs={{0,16},{16,32},{32,48},{48,64},{64,80},{80,96},{96,112},{112,128},... | collective-permute-start | bytes 589832 | tf_op jit(solution)/shard_map/ppermute | solution.py:29
  104.8 5.0 %collective-permute-start.1 = (bf16[2,2,2,8,1536]{4,3,2,1,0:T(8,128)(2,1)S(1)}, bf16[2,2,2,8,1536]{4,3,2,1,0:T(8,128)(2,1)S(1)}, u32[]{:S(2)}, u32[]{:S(2)}) collective-permute-start(bf16[2,2,2,8,1536]{4,3,2,1,0:T(8,128)(2,1)S(1)} %get-tuple-element.21), channel_id=1, source_target_pairs={{16,0},{32,16},{48,32},{64,48},{80,64},{96,80},{112,96},{128,112},... | collective-permute-start | bytes 589832 | tf_op jit(solution)/shard_map/ppermute | solution.py:31
  110.2 14.0 %collective-permute-start.2 = (bf16[2,2,12,2,1536]{4,3,2,1,0:T(2,128)(2,1)S(1)}, bf16[2,2,12,2,1536]{4,3,2,1,0:T(2,128)(2,1)S(1)}, u32[]{:S(2)}, u32[]{:S(2)}) collective-permute-start(bf16[2,2,12,2,1536]{4,3,2,1,0:T(2,128)(2,1)S(1)} %get-tuple-element.16), channel_id=1, source_target_pairs={{0,1},{1,2},{2,3},{3,4},{4,5},{5,6},{6,7},{7,8},{8,9},{9,10},{10,1... | collective-permute-start | bytes 884744 | tf_op jit(solution)/shard_map/ppermute | solution.py:29
  113.8 16.1 %collective-permute-start.3 = (bf16[2,2,12,2,1536]{4,3,2,1,0:T(2,128)(2,1)S(1)}, bf16[2,2,12,2,1536]{4,3,2,1,0:T(2,128)(2,1)S(1)}, u32[]{:S(2)}, u32[]{:S(2)}) collective-permute-start(bf16[2,2,12,2,1536]{4,3,2,1,0:T(2,128)(2,1)S(1)} %get-tuple-element.17), channel_id=1, source_target_pairs={{1,0},{2,1},{3,2},{4,3},{5,4},{6,5},{7,6},{8,7},{9,8},{10,9},{11,1... | collective-permute-start | bytes 884744 | tf_op jit(solution)/shard_map/ppermute | solution.py:31
  133.9 2.2 %copy-start.5 = (bf16[288,12,128]{2,1,0:T(8,128)(2,1)}, bf16[288,12,128]{2,1,0:T(8,128)(2,1)S(1)}, u32[]{:S(2)}) copy-start(bf16[288,12,128]{2,1,0:T(8,128)(2,1)S(1)} %reshape_squeeze.8) | copy-start | bytes 2654212
  133.9 1.7 copy-start.7
  135.6 1.2 copy-start.4
  136.1 1.0 copy-start.2
  149.8 1.7 copy-start.1
  152.3 31.8 %collective-permute-start.4 = (f32[2,2,12,2,1536]{4,3,2,1,0:T(2,128)S(1)}, f32[2,2,12,2,1536]{4,3,2,1,0:T(2,128)S(1)}, u32[]{:S(2)}, u32[]{:S(2)}) collective-permute-start(f32[2,2,12,2,1536]{4,3,2,1,0:T(2,128)S(1)} %get-tuple-element.10), channel_id=1, source_target_pairs={{0,1},{1,2},{2,3},{3,4},{4,5},{5,6},{6,7},{7,8},{8,9},{9,10},{10,1... | collective-permute-start | bytes 1769480 | tf_op jit(solution)/shard_map/ppermute | solution.py:19
  154.2 34.9 %copy-start.3 = (bf16[12,288,128]{2,1,0:T(8,128)(2,1)S(1)}, bf16[12,288,128]{2,1,0:T(8,128)(2,1)}, u32[]{:S(2)}) copy-start(bf16[12,288,128]{2,1,0:T(8,128)(2,1)} %copy-done.2) | copy-start | bytes 2654212
  154.2 34.9 %copy-start.6 = (bf16[288,12,128]{2,1,0:T(8,128)(2,1)S(1)}, bf16[288,12,128]{2,1,0:T(8,128)(2,1)}, u32[]{:S(2)}) copy-start(bf16[288,12,128]{2,1,0:T(8,128)(2,1)} %copy-done.5) | copy-start | bytes 2654212
  154.2 31.4 %collective-permute-start.5 = (f32[2,2,12,2,1536]{4,3,2,1,0:T(2,128)S(1)}, f32[2,2,12,2,1536]{4,3,2,1,0:T(2,128)S(1)}, u32[]{:S(2)}, u32[]{:S(2)}) collective-permute-start(f32[2,2,12,2,1536]{4,3,2,1,0:T(2,128)S(1)} %get-tuple-element.11), channel_id=1, source_target_pairs={{0,15},{1,0},{2,1},{3,2},{4,3},{5,4},{6,5},{7,6},{8,7},{9,8},{10,9... | collective-permute-start | bytes 1769480 | tf_op jit(solution)/shard_map/ppermute | solution.py:19
  186.4 3.3 %copy-start.11 = (bf16[12,128,32]{1,2,0:T(8,128)(2,1)S(1)}, bf16[12,128,32]{1,2,0:T(8,128)(2,1)}, u32[]{:S(2)}) copy-start(bf16[12,128,32]{1,2,0:T(8,128)(2,1)} %copy-done.10) | copy-start | bytes 294916
  187.3 7.5 %collective-permute-start.6 = (f32[2,2,2,8,1536]{4,3,2,1,0:T(8,128)}, f32[2,2,2,8,1536]{4,3,2,1,0:T(8,128)}, u32[]{:S(2)}, u32[]{:S(2)}) collective-permute-start(f32[2,2,2,8,1536]{4,3,2,1,0:T(8,128)} %get-tuple-element.12), channel_id=1, source_target_pairs={{0,16},{16,32},{32,48},{48,64},{64,80},{80,96},{96,112},{112,128},... | collective-permute-start | bytes 1179656 | tf_op jit(solution)/shard_map/ppermute | solution.py:19
  188.6 6.3 %collective-permute-start.7 = (f32[2,2,2,8,1536]{4,3,2,1,0:T(8,128)}, f32[2,2,2,8,1536]{4,3,2,1,0:T(8,128)}, u32[]{:S(2)}, u32[]{:S(2)}) collective-permute-start(f32[2,2,2,8,1536]{4,3,2,1,0:T(8,128)} %get-tuple-element.13), channel_id=1, source_target_pairs={{0,240},{16,0},{32,16},{48,32},{64,48},{80,64},{96,80},{112,96},{1... | collective-permute-start | bytes 1179656 | tf_op jit(solution)/shard_map/ppermute | solution.py:19
Sparse Core Ops, SparseCore 0:
  14.4 84.4 all-gather.5
  104.7 102.0 all-gather.7
